TPU v7x, 32 devices: a whole 2x2x4 slice. The times are simulated.
32 devices in a mesh: row: 16 (over z, x, core), blk: 2 (over y).
Axes of the slice: x: 2, y: 2, z: 4, core: 2. Of those that a mesh axis runs over, the one named last changes fastest.
Arguments:
- embeddings: bfloat16 [8192, 192], P(('row', 'blk')), may hold values from -30 to 30
- vectors: float32 [8192, 16], P(('row', 'blk')), may hold values from -6 to 6
Outputs:
- basis: float32 [8192, 16], P(('row', 'blk'))
- triangle: float32 [16, 16], replicated
All inputs are finite; a program needn't handle non-finite values.
Results may differ from a plain program's by a relative error of at most 0.0088.
Values may be sent and summed in bfloat16 or wider, within the bound.
A program may use at most 64 MiB of HBM per device.

v0:
```python
import functools
import math

import jax
import jax.numpy as jnp
from jax import lax
from jax.experimental import pallas as pl
from jax.experimental.pallas import tpu as pltpu
from jax.sharding import PartitionSpec as P

sharpness = 10.0
epsilon = 1e-06
scale2 = sharpness * math.log2(math.e)
MESH = pl.DeviceIdType.MESH
HIGH = lax.Precision.HIGHEST


def flip(bit, by):
    return bit + by - 2 * bit * by


def split(x):
    high = x.astype(jnp.bfloat16)
    rest = x - high.astype(jnp.float32)
    middle = rest.astype(jnp.bfloat16)
    low = (rest - middle.astype(jnp.float32)).astype(jnp.bfloat16)
    return [high, middle, low]


def kernel(plane_line, emb_hbm, vec_hbm, basis_ref, tri_ref, emb_ref, vec_ref, in_sem,
           rows, cols, turned, aff, dpart, drecv, wts, spart, srecv, gplane, gline,
           row_s, row_r, col_s, col_r, deg_s, deg_r, wt_s, wt_r, sum_s, sum_r, gp_s, gp_r, gl_s, gl_r):
    blk_low, line = plane_line
    n_local = emb_ref.shape[1]
    r = lax.axis_index("row")
    b = lax.axis_index("blk")
    core, x, y = r % 2, (r // 2) % 2, b % 2
    z = (r // 4) * blk_low + b // 2

    def mate(t):
        c2 = flip(core, t & 1)
        x2 = flip(x, (t >> 1) & 1)
        y2 = flip(y, (t >> 2) & 1)
        return ((r // 4) * 4 + x2 * 2 + c2, (b // 2) * 2 + y2)

    def toggled(s):
        total, unit_bit = 0, 1
        while unit_bit < line:
            total = total + unit_bit * flip((z // unit_bit) % 2, (s // unit_bit) % 2)
            unit_bit *= 2
        return total

    def along(s):
        z2 = toggled(s)
        return ((z2 // blk_low) * 4 + x * 2 + core, (z2 % blk_low) * 2 + y)

    emb_in = pltpu.make_async_copy(emb_hbm, emb_ref, in_sem.at[0])
    vec_in = pltpu.make_async_copy(vec_hbm, vec_ref, in_sem.at[1])
    emb_in.start()
    vec_in.start()
    barrier = pltpu.get_barrier_semaphore()
    for t in range(1, 8):
        pl.semaphore_signal(barrier, inc=1, device_id=mate(t), device_id_type=MESH)
    for s in range(1, line):
        pl.semaphore_signal(barrier, inc=1, device_id=along(s), device_id_type=MESH)

    emb_in.wait()
    values = emb_ref[...].astype(jnp.float32)
    norm = lax.rsqrt(jnp.sum(values * values, axis=0, keepdims=True) + epsilon)
    unit = (values * norm).astype(jnp.bfloat16)
    rows[0] = unit
    cols[0] = unit
    pl.semaphore_wait(barrier, 7 + line - 1)

    def send(src, dst, ssem, rsem, to):
        copy = pltpu.make_async_remote_copy(
            src_ref=src, dst_ref=dst, send_sem=ssem, recv_sem=rsem, device_id=to, device_id_type=MESH)
        copy.start()
        return copy

    row_copy = {}
    col_copy = {}
    order = list(range(1, line))
    row_copy[1] = send(rows.at[0], rows.at[1], row_s.at[1], row_r.at[1], mate(1))
    for t in (2, 4, 6):
        row_copy[t] = send(rows.at[0], rows.at[t], row_s.at[t], row_r.at[t], mate(t))
    relayed = line == 4
    half = cols.shape[1] // 2

    def send_part(key, source, slot, start, to):
        part = pl.ds(start, half)
        col_copy[key] = send(cols.at[source, part], cols.at[slot, part], col_s.at[key], col_r.at[key], to)

    if relayed:
        send_part(2, 0, 2, 0, along(2))
        send_part(4, 0, 2, half, along(2))
        col_copy[1] = send(cols.at[0], cols.at[1], col_s.at[1], col_r.at[1], along(1))
        send_part(3, 0, 3, half, along(3))
    else:
        for s in order:
            col_copy[s] = send(cols.at[0], cols.at[s], col_s.at[s], col_r.at[s], along(s))

    def tile(s, t):
        scores = jnp.dot(turned[s], rows[t], preferred_element_type=jnp.float32)
        e = jnp.exp2(scores * scale2 - scale2)
        aff[s, t] = e.astype(jnp.bfloat16)
        part = jnp.sum(e.reshape(n_local // 8, 8, n_local), axis=0)
        return part

    def turn(s):
        turned[s] = cols[s].astype(jnp.float32).T.astype(jnp.bfloat16)

    turn(0)

    def first(t):
        dpart[t] = tile(0, t)

    first(0)
    for t in (1, 2, 4, 6, 3, 5, 7):
        if relayed and t == 6:
            col_copy[2].wait_recv()
            send_part(5, 2, 3, 0, along(1))
        if t in (2, 4, 6):
            row_copy[t].wait_recv()
            row_copy[t + 1] = send(rows.at[t], rows.at[t + 1], row_s.at[t + 1], row_r.at[t + 1], mate(1))
        else:
            row_copy[t].wait_recv()
        first(t)
    for s in order:
        if relayed and s > 1:
            if s == 2:
                col_copy[4].wait_recv()
            else:
                col_copy[3].wait_recv()
                col_copy[5].wait_recv()
        else:
            col_copy[s].wait_recv()
        turn(s)

        def body(t, carry):
            dpart[t] = dpart[t] + tile(s, t)
            return carry

        lax.fori_loop(0, 8, body, 0, unroll=8 if line <= 8 else 1)

    deg_copy = {}
    for t in range(8):
        drecv[8 + t] = jnp.sum(dpart[t], axis=0, keepdims=True)
    for t in range(1, 8):
        deg_copy[t] = send(drecv.at[8 + t], drecv.at[t], deg_s.at[t], deg_r.at[t], mate(t))
    eye = (lax.broadcasted_iota(jnp.int32, (16, 16), 0) == lax.broadcasted_iota(jnp.int32, (16, 16), 1))
    eyef = eye.astype(jnp.float32)
    vec_in.wait()
    vec_t = vec_ref[...]
    degree = drecv[8]
    for t in range(1, 8):
        deg_copy[t].wait_recv()
        degree = degree + drecv[t]
    inverse_root = lax.rsqrt(degree)
    wts[0] = (vec_t * inverse_root).astype(jnp.bfloat16)
    wt_copy = {}
    for s in order:
        wt_copy[s] = send(wts.at[0], wts.at[s], wt_s.at[s], wt_r.at[s], along(s))

    def image(s, t):
        return jnp.dot(wts[s], aff[s, t], preferred_element_type=jnp.float32)

    for t in range(8):
        spart[t] = image(0, t)
    for s in order:
        wt_copy[s].wait_recv()
        for t in range(8):
            spart[t] = spart[t] + image(s, t)
    sum_copy = {}
    for t in range(1, 8):
        sum_copy[t] = send(spart.at[t], srecv.at[t], sum_s.at[t], sum_r.at[t], mate(t))
    summed = spart[0]
    for t in range(1, 8):
        sum_copy[t].wait_recv()
        summed = summed + srecv[t]
    projected = summed * inverse_root
    pieces = jnp.concatenate(split(projected), axis=0)
    products = lax.dot_general(pieces, pieces, (((1,), (1,)), ((), ())),
                               preferred_element_type=jnp.float32)
    halves = products[0:16] + products[16:32] + products[32:48]
    gram = halves[:, 0:16] + halves[:, 16:32] + halves[:, 32:48]
    gram = jnp.concatenate([gram[0:8], gram[8:16]], axis=1)
    gplane[0] = gram
    gp_copy = {}
    for t in range(1, 8):
        gp_copy[t] = send(gplane.at[0], gplane.at[t], gp_s.at[t], gp_r.at[t], mate(t))
    for t in range(1, 8):
        gp_copy[t].wait_recv()
    total = ((gram + gplane[1]) + (gplane[2] + gplane[3])) + ((gplane[4] + gplane[5]) + (gplane[6] + gplane[7]))
    gline[0] = total
    gl_copy = {}
    for s in order:
        gl_copy[s] = send(gline.at[0], gline.at[s], gl_s.at[s], gl_r.at[s], along(s))
    for s in order:
        gl_copy[s].wait_recv()
    terms = [gline[s] for s in range(line)]
    while len(terms) > 1:
        terms = [terms[k] + terms[k + 1] for k in range(0, len(terms), 2)]
    a = jnp.concatenate([terms[0][:, 0:16], terms[0][:, 16:32]], axis=0)

    m = eyef
    below = lax.broadcasted_iota(jnp.int32, (16, 1), 0)
    for k in range(16):
        f = jnp.where(below > k, a[:, k:k + 1] / a[k:k + 1, k:k + 1], 0.0)
        a = a - f * a[k:k + 1, :]
        m = m - f * m[k:k + 1, :]
    root = lax.rsqrt(jnp.sum(jnp.where(eye, a, 0.0), axis=1, keepdims=True))
    upper = lax.broadcasted_iota(jnp.int32, (16, 16), 0) <= lax.broadcasted_iota(jnp.int32, (16, 16), 1)
    tri_ref[...] = jnp.where(upper, a * root, 0.0)
    basis_ref[...] = jnp.dot(m * root, projected, precision=HIGH, preferred_element_type=jnp.float32)

    for group in (row_copy, col_copy, deg_copy, wt_copy, sum_copy, gp_copy, gl_copy):
        for copy in group.values():
            copy.wait_send()


def per_device(sizes, embeddings, vectors):
    blk_low, line = sizes
    n, dim = embeddings.shape
    k = vectors.shape[1]
    dma = pltpu.SemaphoreType.DMA
    vmem = pl.BlockSpec(memory_space=pltpu.VMEM)
    basis_t, tri = pl.pallas_call(
        functools.partial(kernel, sizes),
        out_shape=(jax.ShapeDtypeStruct((k, n), jnp.float32), jax.ShapeDtypeStruct((k, k), jnp.float32)),
        in_specs=[pl.BlockSpec(memory_space=pl.ANY)] * 2,
        out_specs=(vmem, vmem),
        scratch_shapes=[
            pltpu.VMEM((dim, n), jnp.bfloat16),
            pltpu.VMEM((k, n), jnp.float32),
            dma((2,)),
            pltpu.VMEM((8, dim, n), jnp.bfloat16),
            pltpu.VMEM((line, dim, n), jnp.bfloat16),
            pltpu.VMEM((line, n, dim), jnp.bfloat16),
            pltpu.VMEM((line, 8, n, n), jnp.bfloat16),
            pltpu.VMEM((8, 8, n), jnp.float32),
            pltpu.VMEM((16, 1, n), jnp.float32),
            pltpu.VMEM((line, k, n), jnp.bfloat16),
            pltpu.VMEM((8, k, n), jnp.float32),
            pltpu.VMEM((8, k, n), jnp.float32),
            pltpu.VMEM((8, k // 2, 2 * k), jnp.float32),
            pltpu.VMEM((line, k // 2, 2 * k), jnp.float32),
            dma((8,)), dma((8,)), dma((line + 2,)), dma((line + 2,)), dma((8,)), dma((8,)),
            dma((line,)), dma((line,)), dma((8,)), dma((8,)), dma((8,)), dma((8,)),
            dma((line,)), dma((line,)),
        ],
        compiler_params=pltpu.CompilerParams(
            collective_id=0, has_side_effects=True, vmem_limit_bytes=60 * 1024 * 1024),
        name="cluster",
    )(embeddings.T, vectors.T)
    return basis_t.T, tri


def solution(mesh):
    blk_low = mesh.shape["blk"] // 2
    line = (mesh.shape["row"] // 4) * blk_low
    placed = (P(("row", "blk"), None), P(("row", "blk"), None))
    return jax.shard_map(
        functools.partial(per_device, (blk_low, line)),
        mesh=mesh,
        in_specs=placed,
        out_specs=(P(("row", "blk"), None), P()),
        check_vma=False,
    )
```

profile of v0, /device:TPU:0, one launch (start us, length us, event | category | flops | bytes accessed | tf_op | source)
XLA Modules:
  0.0 38.0 jit_solution(14452250505313681868)
XLA Ops:
  0.6 35.4 %cluster.1 = (f32[16,256]{1,0:T(8,128)}, f32[16,16]{1,0:T(8,128)}) custom-call(bf16[192,256]{1,0:T(8,128)(2,1)} %bitcast.3, f32[16,256]{1,0:T(8,128)} %bitcast.4), custom_call_target="tpu_custom_call" | custom-call | tf_op jit(solution)/shard_map/cluster/pallas_call | solution.py:228
  36.0 0.0 copy-start
  36.0 1.3 %copy.6 = f32[256,16]{0,1:T(8,128)} copy(f32[256,16]{0,1:T(8,128)} %bitcast.5) | data formatting | bytes 32768
  37.4 0.0 copy-done
  37.4 0.6 %copy.7 = f32[16,16]{1,0:T(8,128)} copy(f32[16,16]{1,0:T(8,128)S(1)} %copy-done) | data formatting | bytes 2048
Async XLA Ops:
  36.0 1.3 %copy-start = (f32[16,16]{1,0:T(8,128)S(1)}, f32[16,16]{1,0:T(8,128)}, u32[]{:S(2)}) copy-start(f32[16,16]{1,0:T(8,128)} %get-tuple-element.9) | copy-start | bytes 3076
where the time goes:
time: 38.2 us; the launch traced here: 38 us
  Pallas kernels  35.4 us (93%)
  local copies, waits for them, and re-layouts  1.93 us (5%)
  between operations  0.65 us (2%)
    pallas_call x1, Pallas kernels, per_device(): pl.pallas_call(functools.partial(kernel, sizes), out_shape=(jax.ShapeDtyp...  35.4 us
    unnamed x4, local copies, waits for them, and re-layouts  1.93 us

commit v1 on v0

v1 whole, which is shorter than its diff:
```python
import functools
import math

import jax
import jax.numpy as jnp
from jax import lax
from jax.experimental import pallas as pl
from jax.experimental.pallas import tpu as pltpu
from jax.sharding import PartitionSpec as P

sharpness = 10.0
epsilon = 1e-06
scale2 = sharpness * math.log2(math.e)
MESH = pl.DeviceIdType.MESH
HIGH = lax.Precision.HIGHEST
TRANS = (((1,), (1,)), ((), ()))


def flip(bit, by):
    return bit + by - 2 * bit * by


def swap(x, bit):
    if bit == 4:
        return pltpu.roll(x, 4, 0)
    row = lax.broadcasted_iota(jnp.int32, x.shape, 0)
    return jnp.where((row & bit) == 0, pltpu.roll(x, 8 - bit, 0), pltpu.roll(x, bit, 0))


def pair_sum(x):
    while x.shape[0] > 1:
        x = x.reshape(x.shape[0] // 2, 2, *x.shape[1:])
        x = x[:, 0] + x[:, 1]
    return x[0]


def kernel(plane_line, emb_hbm, vec_hbm, basis_ref, tri_ref, emb_ref, in_sem,
           rows, cols, turned, aff, vecs, dpart, dsend, drecv, wts, spart, srecv, gsend, grecv,
           row_s, row_r, col_s, col_r, vec_s, vec_r, deg_s, deg_r, sum_s, sum_r, g_s, g_r):
    blk_low, line = plane_line
    n_local = emb_ref.shape[1]
    k = vecs.shape[1]
    r = lax.axis_index("row")
    b = lax.axis_index("blk")
    core, x, y = r % 2, (r // 2) % 2, b % 2
    z = (r // 4) * blk_low + b // 2

    def toggled(s):
        total, unit_bit = 0, 1
        while unit_bit < line:
            total = total + unit_bit * flip((z // unit_bit) % 2, (s // unit_bit) % 2)
            unit_bit *= 2
        return total

    def peer(s, t):
        c2 = flip(core, t % 2)
        x2 = flip(x, (t // 2) % 2)
        y2 = flip(y, (t // 4) % 2)
        z2 = toggled(s)
        return ((z2 // blk_low) * 4 + x2 * 2 + c2, (z2 % blk_low) * 2 + y2)

    def mate(t):
        return peer(0, t)

    def along(s):
        return peer(s, 0)

    emb_in = pltpu.make_async_copy(emb_hbm, emb_ref, in_sem.at[0])
    vec_in = pltpu.make_async_copy(vec_hbm, vecs.at[0], in_sem.at[1])
    emb_in.start()
    vec_in.start()
    barrier = pltpu.get_barrier_semaphore()
    for t in range(1, 8):
        pl.semaphore_signal(barrier, inc=1, device_id=mate(t), device_id_type=MESH)
    for s in range(1, line):
        pl.semaphore_signal(barrier, inc=1, device_id=along(s), device_id_type=MESH)

    emb_in.wait()
    values = emb_ref[...].astype(jnp.float32)
    norm = lax.rsqrt(jnp.sum(values * values, axis=0, keepdims=True) + epsilon)
    unit = (values * norm).astype(jnp.bfloat16)
    rows[0] = unit
    cols[0] = unit
    vec_in.wait()
    pl.semaphore_wait(barrier, 7 + line - 1)

    def send(src, dst, ssem, rsem, to):
        copy = pltpu.make_async_remote_copy(
            src_ref=src, dst_ref=dst, send_sem=ssem, recv_sem=rsem, device_id=to, device_id_type=MESH)
        copy.start()
        return copy

    row_copy = {}
    col_copy = {}
    vec_copy = {}
    order = list(range(1, line))
    relayed = line == 4
    half = cols.shape[1] // 2

    def send_row(t, source=0, to=None):
        row_copy[t] = send(rows.at[source], rows.at[t], row_s.at[t], row_r.at[t], mate(t if to is None else to))

    def send_vec(t, source=0, to=None):
        vec_copy[t] = send(vecs.at[source], vecs.at[t], vec_s.at[t], vec_r.at[t], mate(t if to is None else to))

    def send_part(key, source, slot, start, to):
        part = pl.ds(start, half)
        col_copy[key] = send(cols.at[source, part], cols.at[slot, part], col_s.at[key], col_r.at[key], to)

    send_row(1)
    for t in (2, 4, 6):
        send_row(t)
    if relayed:
        send_part(2, 0, 2, 0, along(2))
        send_part(4, 0, 2, half, along(2))
        col_copy[1] = send(cols.at[0], cols.at[1], col_s.at[1], col_r.at[1], along(1))
        send_part(3, 0, 3, half, along(3))
    else:
        for s in order:
            col_copy[s] = send(cols.at[0], cols.at[s], col_s.at[s], col_r.at[s], along(s))
    for t in (1, 2, 4, 6):
        send_vec(t)

    def tile(s, t):
        scores = jnp.dot(turned[s], rows[t], preferred_element_type=jnp.float32)
        e = jnp.exp2(scores * scale2 - scale2)
        aff[s, t] = e.astype(jnp.bfloat16)
        return jnp.sum(e.reshape(n_local // 8, 8, n_local), axis=0)

    def turn(s):
        turned[s] = cols[s].astype(jnp.float32).T.astype(jnp.bfloat16)

    have_rows, have_cols = [], []

    def do_tile(s, t):
        if len(have_cols) == 1:
            dpart[t] = tile(s, t)
        else:
            dpart[t] = dpart[t] + tile(s, t)

    def row_here(t):
        if t:
            row_copy[t].wait_recv()
            if t in (2, 4, 6):
                send_row(t + 1, source=t, to=1)
        have_rows.append(t)
        for s in have_cols:
            if s == 0:
                dpart[t] = tile(0, t)
            else:
                dpart[t] = dpart[t] + tile(s, t)

    def col_here(s):
        turn(s)
        have_cols.append(s)
        for t in have_rows:
            dpart[t] = dpart[t] + tile(s, t)

    turn(0)
    have_cols.append(0)
    row_here(0)
    if relayed:
        row_here(1)
        row_here(2)
        row_here(4)
        col_copy[2].wait_recv()
        send_part(5, 2, 3, 0, along(1))
        row_here(3)
        row_here(5)
        col_copy[1].wait_recv()
        col_here(1)
        row_here(6)
        col_copy[4].wait_recv()
        col_here(2)
        row_here(7)
        col_copy[3].wait_recv()
        col_copy[5].wait_recv()
        col_here(3)
    else:
        for t in (1, 2, 4, 6, 3, 5, 7):
            row_here(t)
        for s in order:
            col_copy[s].wait_recv()
            turn(s)

            def body(t, carry):
                dpart[t] = dpart[t] + tile(s, t)
                return carry

            lax.fori_loop(0, 8, body, 0)

    dsend[...] = jnp.concatenate([jnp.sum(dpart[t], axis=0, keepdims=True) for t in range(8)], axis=0)
    deg_copy = {}
    for t in (7, 6, 5, 4, 3, 2, 1):
        deg_copy[t] = send(dsend, drecv.at[t], deg_s.at[t], deg_r.at[t], mate(t))
    for t in (2, 4, 6):
        vec_copy[t].wait_recv()
        send_vec(t + 1, source=t, to=1)
    parts = [dsend[...]]
    for t in range(1, 8):
        deg_copy[t].wait_recv()
        parts.append(drecv[t])
    for bit in (1, 2, 4):
        parts = [parts[i] + swap(parts[i + 1], bit) for i in range(0, len(parts), 2)]
    inverse_root = lax.rsqrt(parts[0])
    for t in (1, 3, 5, 7):
        vec_copy[t].wait_recv()
    for t in range(8):
        wts[:, t * n_local:(t + 1) * n_local] = (vecs[t] * inverse_root[t:t + 1, :]).astype(jnp.bfloat16)

    def image(s):
        total = None
        for t in range(8):
            part = lax.dot_general(aff[s, t], wts[:, t * n_local:(t + 1) * n_local], TRANS,
                                   preferred_element_type=jnp.float32)
            total = part if total is None else total + part
        return total.T

    sum_copy = {}
    for s in reversed(order):
        spart[s] = image(s)
        sum_copy[s] = send(spart.at[s], srecv.at[s], sum_s.at[s], sum_r.at[s], along(s))
    terms = [image(0)]
    for s in order:
        sum_copy[s].wait_recv()
        terms.append(srecv[s])
    while len(terms) > 1:
        terms = [terms[i] + terms[i + 1] for i in range(0, len(terms), 2)]
    projected = terms[0] * inverse_root[0:1, :]
    gram = lax.dot_general(projected, projected, TRANS, precision=HIGH, preferred_element_type=jnp.float32)
    wide = jnp.concatenate([gram, jnp.zeros((k, 128 - k), jnp.float32)], axis=1)
    wide = jnp.concatenate([pltpu.roll(wide[h:h + 8], 0, 1, stride=k, stride_axis=0) for h in (0, 8)], axis=0)
    gsend[...] = jnp.sum(wide.reshape(2, 8, 128), axis=1)
    grecv[0] = gsend[...]
    g_copy = {}
    for s in reversed(range(line)):
        for t in reversed(range(8)):
            if s or t:
                i = s * 8 + t
                g_copy[i] = send(gsend, grecv.at[i], g_s.at[i], g_r.at[i], peer(s, t))
    for i in range(1, 8 * line):
        g_copy[i].wait_recv()
    total = pair_sum(grecv[...])
    lane = lax.broadcasted_iota(jnp.int32, (16, 128), 1)
    below = lax.broadcasted_iota(jnp.int32, (16, 128), 0)
    flat = jnp.concatenate([jnp.broadcast_to(total[h:h + 1], (8, 128)) for h in (0, 1)], axis=0)
    square = [pltpu.roll(flat[h:h + 8], k, 1, stride=k, stride_axis=0) for h in (0, 8)]
    square = jnp.concatenate([swap(swap(swap(q, 1), 2), 4) for q in square], axis=0)
    a = [jnp.broadcast_to(square[:, j:j + 1], (16, 128)) for j in range(k)]
    m = projected
    pivot = jnp.zeros((16, 128), jnp.float32)
    for i in range(k):
        head = a[i][i:i + 1]
        pivot = jnp.where(below == i, head, pivot)
        f = jnp.where(below > i, a[i] * (1.0 / head), 0.0)
        for j in range(i + 1, k):
            a[j] = a[j] - f * a[j][i:i + 1]
        m = m - jnp.concatenate([f] * (n_local // 128), axis=1) * m[i:i + 1]
    root = lax.rsqrt(pivot)
    tri = jnp.zeros((16, 128), jnp.float32)
    for j in range(k):
        tri = jnp.where((lane == j) & (below <= j), a[j], tri)
    tri_ref[...] = (tri * root)[:, :k]
    basis_ref[...] = m * jnp.concatenate([root] * (n_local // 128), axis=1)

    for group in (row_copy, col_copy, vec_copy, deg_copy, sum_copy, g_copy):
        for copy in group.values():
            copy.wait_send()


def per_device(sizes, embeddings, vectors):
    blk_low, line = sizes
    n, dim = embeddings.shape
    k = vectors.shape[1]
    dma = pltpu.SemaphoreType.DMA
    vmem = pl.BlockSpec(memory_space=pltpu.VMEM)
    basis_t, tri = pl.pallas_call(
        functools.partial(kernel, sizes),
        out_shape=(jax.ShapeDtypeStruct((k, n), jnp.float32), jax.ShapeDtypeStruct((k, k), jnp.float32)),
        in_specs=[pl.BlockSpec(memory_space=pltpu.HBM)] * 2,
        out_specs=(vmem, vmem),
        scratch_shapes=[
            pltpu.VMEM((dim, n), jnp.bfloat16),
            dma((2,)),
            pltpu.VMEM((8, dim, n), jnp.bfloat16),
            pltpu.VMEM((line, dim, n), jnp.bfloat16),
            pltpu.VMEM((line, n, dim), jnp.bfloat16),
            pltpu.VMEM((line, 8, n, n), jnp.bfloat16),
            pltpu.VMEM((8, k, n), jnp.float32),
            pltpu.VMEM((8, 8, n), jnp.float32),
            pltpu.VMEM((8, n), jnp.float32),
            pltpu.VMEM((8, 8, n), jnp.float32),
            pltpu.VMEM((k, 8 * n), jnp.bfloat16),
            pltpu.VMEM((line, k, n), jnp.float32),
            pltpu.VMEM((line, k, n), jnp.float32),
            pltpu.VMEM((2, 128), jnp.float32),
            pltpu.VMEM((8 * line, 2, 128), jnp.float32),
            dma((8,)), dma((8,)), dma((line + 2,)), dma((line + 2,)), dma((8,)), dma((8,)),
            dma((8,)), dma((8,)), dma((line,)), dma((line,)), dma((8 * line,)), dma((8 * line,)),
        ],
        compiler_params=pltpu.CompilerParams(
            collective_id=0, has_side_effects=True, vmem_limit_bytes=(16 if line <= 8 else 60) * 1024 * 1024),
        name="cluster",
    )(embeddings.T, vectors.T)
    return basis_t.T, tri


def solution(mesh):
    blk_low = mesh.shape["blk"] // 2
    line = (mesh.shape["row"] // 4) * blk_low
    placed = (P(("row", "blk"), None), P(("row", "blk"), None))
    return jax.shard_map(
        functools.partial(per_device, (blk_low, line)),
        mesh=mesh,
        in_specs=placed,
        out_specs=(P(("row", "blk"), None), P()),
        check_vma=False,
    )
```

time: 38.2 us -> 33.7 us (0.88)
  Pallas kernels: 35.4 us -> 30 us
  local copies, waits for them, and re-layouts: 1.93 us -> 2.81 us
    pallas_call x1, Pallas kernels: 35.4 us -> 30 us  [per_device(): pl.pallas_call(functools.partial(kernel, sizes), out_shape=(jax.ShapeDtyp...]
    unnamed x4 -> x6, local copies, waits for them, and re-layouts: 1.93 us -> 2.81 us
where the time goes in v1:
time: 33.7 us; the launch traced here: 33.4 us
  Pallas kernels  30 us (89%)
  local copies, waits for them, and re-layouts  2.81 us (8%)
  between operations  0.65 us (2%)
    pallas_call x1, Pallas kernels, per_device(): pl.pallas_call(functools.partial(kernel, sizes), out_shape=(jax.ShapeDtyp...  30 us
    unnamed x6, local copies, waits for them, and re-layouts  2.81 us

profile of v1, /device:TPU:0, one launch (start us, length us, event | category | flops | bytes accessed | tf_op | source)
XLA Modules:
  0.0 33.4 jit_solution(7171731624641758123)
XLA Ops:
  0.6 0.0 copy-start
  0.6 0.9 %copy-done = bf16[256,192]{0,1:T(8,128)(2,1)S(1)} copy-done((bf16[256,192]{0,1:T(8,128)(2,1)S(1)}, bf16[256,192]{0,1:T(8,128)(2,1)}, u32[]{:S(2)}) %copy-start) | copy-done | bytes 98328
  1.5 0.0 copy-start.1
  1.5 0.7 %copy-done.1 = f32[256,16]{0,1:T(8,128)S(1)} copy-done((f32[256,16]{0,1:T(8,128)S(1)}, f32[256,16]{0,1:T(8,128)}, u32[]{:S(2)}) %copy-start.1) | copy-done | bytes 16408
  2.2 30.0 %cluster.1 = (f32[16,256]{1,0:T(8,128)S(1)}, f32[16,16]{1,0:T(8,128)S(1)}) custom-call(bf16[192,256]{1,0:T(8,128)(2,1)S(1)} %bitcast.3, f32[16,256]{1,0:T(8,128)S(1)} %bitcast.4), custom_call_target="tpu_custom_call" | custom-call | tf_op jit(solution)/shard_map/cluster/pallas_call | solution.py:277
  32.2 0.6 %copy.6 = f32[256,16]{0,1:T(8,128)} copy(f32[256,16]{0,1:T(8,128)S(1)} %bitcast.5) | data formatting | bytes 32768
  32.8 0.6 %copy.7 = f32[16,16]{1,0:T(8,128)} copy(f32[16,16]{1,0:T(8,128)S(1)} %get-tuple-element.9) | data formatting | bytes 2048
Async XLA Ops:
  0.6 0.9 %copy-start = (bf16[256,192]{0,1:T(8,128)(2,1)S(1)}, bf16[256,192]{0,1:T(8,128)(2,1)}, u32[]{:S(2)}) copy-start(bf16[256,192]{0,1:T(8,128)(2,1)} %param.2) | copy-start | bytes 294916
  1.5 0.7 %copy-start.1 = (f32[256,16]{0,1:T(8,128)S(1)}, f32[256,16]{0,1:T(8,128)}, u32[]{:S(2)}) copy-start(f32[256,16]{0,1:T(8,128)} %param.3) | copy-start | bytes 49156

commit v2 on v1

--- a/solution.py
+++ b/solution.py
@@ -12,7 +12,6 @@
 epsilon = 1e-06
 scale2 = sharpness * math.log2(math.e)
 MESH = pl.DeviceIdType.MESH
-HIGH = lax.Precision.HIGHEST
 TRANS = (((1,), (1,)), ((), ()))
 
 
@@ -25,6 +24,14 @@
         return pltpu.roll(x, 4, 0)
     row = lax.broadcasted_iota(jnp.int32, x.shape, 0)
     return jnp.where((row & bit) == 0, pltpu.roll(x, 8 - bit, 0), pltpu.roll(x, bit, 0))
+
+
+def split(x):
+    high = x.astype(jnp.bfloat16)
+    rest = x - high.astype(jnp.float32)
+    middle = rest.astype(jnp.bfloat16)
+    low = (rest - middle.astype(jnp.float32)).astype(jnp.bfloat16)
+    return high, middle, low
 
 
 def pair_sum(x):
@@ -95,7 +102,7 @@
     vec_copy = {}
     order = list(range(1, line))
     relayed = line == 4
-    half = cols.shape[1] // 2
+    half = n_local // 2
 
     def send_row(t, source=0, to=None):
         row_copy[t] = send(rows.at[source], rows.at[t], row_s.at[t], row_r.at[t], mate(t if to is None else to))
@@ -105,11 +112,8 @@
 
     def send_part(key, source, slot, start, to):
         part = pl.ds(start, half)
-        col_copy[key] = send(cols.at[source, part], cols.at[slot, part], col_s.at[key], col_r.at[key], to)
-
-    send_row(1)
-    for t in (2, 4, 6):
-        send_row(t)
+        col_copy[key] = send(cols.at[source, :, part], cols.at[slot, :, part], col_s.at[key], col_r.at[key], to)
+
     if relayed:
         send_part(2, 0, 2, 0, along(2))
         send_part(4, 0, 2, half, along(2))
@@ -118,6 +122,8 @@
     else:
         for s in order:
             col_copy[s] = send(cols.at[0], cols.at[s], col_s.at[s], col_r.at[s], along(s))
+    for t in (2, 4, 6, 1):
+        send_row(t)
     for t in (1, 2, 4, 6):
         send_vec(t)
 
@@ -132,17 +138,14 @@
 
     have_rows, have_cols = [], []
 
-    def do_tile(s, t):
-        if len(have_cols) == 1:
-            dpart[t] = tile(s, t)
-        else:
-            dpart[t] = dpart[t] + tile(s, t)
-
-    def row_here(t):
-        if t:
-            row_copy[t].wait_recv()
-            if t in (2, 4, 6):
-                send_row(t + 1, source=t, to=1)
+    def row_in(t):
+        row_copy[t].wait_recv()
+        if t in (2, 4, 6):
+            send_row(t + 1, source=t, to=1)
+
+    def row_here(t, wait=True):
+        if t and wait:
+            row_in(t)
         have_rows.append(t)
         for s in have_cols:
             if s == 0:
@@ -156,26 +159,37 @@
         for t in have_rows:
             dpart[t] = dpart[t] + tile(s, t)
 
+    def half_here(s, start):
+        part = slice(start, start + half)
+        turned[s, part] = cols[s, :, part].astype(jnp.float32).T.astype(jnp.bfloat16)
+        for t in range(8):
+            scores = jnp.dot(turned[s, part], rows[t], preferred_element_type=jnp.float32)
+            e = jnp.exp2(scores * scale2 - scale2)
+            aff[s, t, part] = e.astype(jnp.bfloat16)
+            dpart[t] = dpart[t] + jnp.sum(e.reshape(half // 8, 8, n_local), axis=0)
+
     turn(0)
     have_cols.append(0)
     row_here(0)
     if relayed:
         row_here(1)
+        col_copy[2].wait_recv()
+        send_part(5, 2, 3, 0, along(1))
         row_here(2)
         row_here(4)
-        col_copy[2].wait_recv()
-        send_part(5, 2, 3, 0, along(1))
         row_here(3)
         row_here(5)
+        row_in(6)
         col_copy[1].wait_recv()
         col_here(1)
-        row_here(6)
+        row_here(6, False)
         col_copy[4].wait_recv()
         col_here(2)
         row_here(7)
         col_copy[3].wait_recv()
+        half_here(3, half)
         col_copy[5].wait_recv()
-        col_here(3)
+        half_here(3, 0)
     else:
         for t in (1, 2, 4, 6, 3, 5, 7):
             row_here(t)
@@ -227,7 +241,10 @@
     while len(terms) > 1:
         terms = [terms[i] + terms[i + 1] for i in range(0, len(terms), 2)]
     projected = terms[0] * inverse_root[0:1, :]
-    gram = lax.dot_general(projected, projected, TRANS, precision=HIGH, preferred_element_type=jnp.float32)
+    high, middle, low = split(projected)
+    left = jnp.concatenate([high, high, middle, middle, high, low], axis=1)
+    right = jnp.concatenate([high, middle, high, middle, low, high], axis=1)
+    gram = lax.dot_general(left, right, TRANS, preferred_element_type=jnp.float32)
     wide = jnp.concatenate([gram, jnp.zeros((k, 128 - k), jnp.float32)], axis=1)
     wide = jnp.concatenate([pltpu.roll(wide[h:h + 8], 0, 1, stride=k, stride_axis=0) for h in (0, 8)], axis=0)
     gsend[...] = jnp.sum(wide.reshape(2, 8, 128), axis=1)
@@ -268,6 +285,15 @@
             copy.wait_send()
 
 
+def store(basis_ref, tri_ref, basis_hbm, tri_hbm, sem):
+    copies = [pltpu.make_async_copy(basis_ref, basis_hbm, sem.at[0]),
+              pltpu.make_async_copy(tri_ref, tri_hbm, sem.at[1])]
+    for copy in copies:
+        copy.start()
+    for copy in copies:
+        copy.wait()
+
+
 def per_device(sizes, embeddings, vectors):
     blk_low, line = sizes
     n, dim = embeddings.shape
@@ -299,9 +325,18 @@
             dma((8,)), dma((8,)), dma((line,)), dma((line,)), dma((8 * line,)), dma((8 * line,)),
         ],
         compiler_params=pltpu.CompilerParams(
-            collective_id=0, has_side_effects=True, vmem_limit_bytes=(16 if line <= 8 else 60) * 1024 * 1024),
+            collective_id=0, has_side_effects=True, vmem_limit_bytes=56524800),
         name="cluster",
     )(embeddings.T, vectors.T)
+    basis_t, tri = pl.pallas_call(
+        store,
+        out_shape=(jax.ShapeDtypeStruct((k, n), jnp.float32), jax.ShapeDtypeStruct((k, k), jnp.float32)),
+        in_specs=[vmem] * 2,
+        out_specs=[pl.BlockSpec(memory_space=pl.ANY)] * 2,
+        scratch_shapes=[dma((2,))],
+        compiler_params=pltpu.CompilerParams(vmem_limit_bytes=1024 * 1024),
+        name="store",
+    )(basis_t, tri)
     return basis_t.T, tri
 
 

time: 33.7 us -> 30.9 us (0.917)
  local copies, waits for them, and re-layouts: 2.81 us -> 0 us
    unnamed x6 -> x0, local copies, waits for them, and re-layouts: 2.81 us -> none
    pallas_call x0 -> x1, Pallas kernels: none -> 0.63 us  [per_device(): pl.pallas_call(store, out_shape=(jax.ShapeDtypeStruct((k, n), jnp.float32...]
    pallas_call x1, Pallas kernels: 30 us -> 29.5 us  [per_device(): pl.pallas_call(functools.partial(kernel, sizes), out_shape=(jax.ShapeDtyp...]
where the time goes in v2:
time: 30.9 us; the launch traced here: 30.7 us
  Pallas kernels  30.1 us (97%)
  between operations  0.64 us (2%)
    pallas_call x1, Pallas kernels, per_device(): pl.pallas_call(functools.partial(kernel, sizes), out_shape=(jax.ShapeDtyp...  29.5 us
    pallas_call x1, Pallas kernels, per_device(): pl.pallas_call(store, out_shape=(jax.ShapeDtypeStruct((k, n), jnp.float32...  0.63 us

profile of v2, /device:TPU:0, one launch (start us, length us, event | category | flops | bytes accessed | tf_op | source)
XLA Modules:
  0.0 30.7 jit_solution(7779489932379884423)
XLA Ops:
  0.6 29.5 %cluster.1 = (f32[16,256]{1,0:T(8,128)S(1)}, f32[16,16]{1,0:T(8,128)S(1)}) custom-call(bf16[192,256]{1,0:T(8,128)(2,1)} %bitcast.3, f32[16,256]{1,0:T(8,128)} %bitcast.4), custom_call_target="tpu_custom_call" | custom-call | tf_op jit(solution)/shard_map/cluster/pallas_call | solution.py:303
  30.1 0.6 %store.1 = (f32[16,256]{1,0:T(8,128)}, f32[16,16]{1,0:T(8,128)}) custom-call(f32[16,256]{1,0:T(8,128)S(1)} %get-tuple-element.6.basis_ref, f32[16,16]{1,0:T(8,128)S(1)} %get-tuple-element.7.tri_ref), custom_call_target="tpu_custom_call" | custom-call | tf_op jit(solution)/shard_map/store/pallas_call | solution.py:331
